TPU v7x, 32 devices: a whole 2x2x4 slice. The times are simulated.
32 devices in a mesh: dp: 16 (over z, x, core), mp: 2 (over y).
Axes of the slice: x: 2, y: 2, z: 4, core: 2. Of those that a mesh axis runs over, the one named last changes fastest.
Arguments:
- tokens: bfloat16 [192, 4608], P('dp', 'mp'), may hold values from -6 to 6
- frozen_weight: bfloat16 [2, 4608, 36864], P(None, 'mp', 'dp'), may hold values from -36 to 36
- adapter_down: bfloat16 [2, 16, 4608], P(None, None, 'mp'), may hold values from -1.5 to 1.5
- adapter_up: bfloat16 [2, 16, 36864], P(None, None, 'dp'), may hold values from -3 to 3
- magnitude: float32 [2, 36864], P(None, 'dp'), may hold values from 0.5 to 2
- hidden_gradient: bfloat16 [192, 36864], P('mp', 'dp'), may hold values from -0.59765625 to 0.59765625
Outputs:
- hidden: bfloat16 [192, 36864], P('mp', 'dp')
- token_gradient: float32 [192, 4608], P('dp', 'mp')
- adapter_down_gradient: float32 [2, 16, 4608], P(None, None, 'mp')
- adapter_up_gradient: float32 [2, 16, 36864], P(None, None, 'dp')
- magnitude_gradient: float32 [2, 36864], P(None, 'dp')
All inputs are finite; a program needn't handle non-finite values.
Results may differ from a plain program's by a relative error of at most 0.023.
Values may be sent and summed in bfloat16 or wider, within the bound.
A program may use at most 64 MiB of HBM per device.

v0:
```python
import jax
import jax.numpy as jnp
from jax import lax
from jax.sharding import PartitionSpec as P

LOWRANK_SCALE = 2.0
EPSILON = 1e-06
MATMUL_ACCURACY = lax.Precision.HIGHEST


def gelu_pair(source):
    cubic_term = source + 0.044715 * source * source * source
    tangent = jnp.tanh(0.7978845608028654 * cubic_term)
    result = 0.5 * source * (1.0 + tangent)
    derivative = 0.5 * (1.0 + tangent) + 0.5 * source * (
        1.0 - tangent * tangent
    ) * 0.7978845608028654 * (1.0 + 0.134145 * source * source)
    return (result, derivative)


def on_device(tokens, frozen_weight, adapter_down, adapter_up, magnitude, hidden_gradient):
    every_row = lax.all_gather(tokens, "dp", axis=0, tiled=True)
    down_broad = adapter_down.astype(jnp.float32)
    up_broad = adapter_up.astype(jnp.float32)
    base_square = jnp.sum(jnp.square(frozen_weight.astype(jnp.float32)), axis=1)
    cross_base = jnp.einsum(
        "krd,kdf->krf", adapter_down, frozen_weight, preferred_element_type=jnp.float32
    )
    gram_part = jnp.einsum(
        "krd,ksd->krs", adapter_down, adapter_down, preferred_element_type=jnp.float32
    )
    square_base, cross_total, gram_sum = (
        lax.psum(base_square.astype(jnp.bfloat16), "mp").astype(jnp.float32),
        lax.psum(cross_base.astype(jnp.bfloat16), "mp").astype(jnp.float32),
        lax.psum(gram_part.astype(jnp.bfloat16), "mp").astype(jnp.float32),
    )
    gram_up = jnp.einsum("krs,ksf->krf", gram_sum, up_broad, precision=MATMUL_ACCURACY)
    mixed_sum = cross_total + LOWRANK_SCALE * gram_up
    square_sum = (
        square_base
        + 2.0 * LOWRANK_SCALE * jnp.sum(up_broad * cross_total, axis=1)
        + LOWRANK_SCALE * LOWRANK_SCALE * jnp.sum(up_broad * gram_up, axis=1)
    )
    base_part = jnp.einsum(
        "td,kdf->ktf", every_row, frozen_weight, preferred_element_type=jnp.float32
    )
    lowrank_piece = jnp.einsum(
        "su,vgu->vsg", every_row, adapter_down, preferred_element_type=jnp.float32
    )
    col_norm = jnp.sqrt(square_sum + EPSILON)
    col_ratio = magnitude / col_norm
    share_rows = every_row.shape[0] // lax.axis_size("mp")
    base_sum, low_sum = (
        lax.psum(base_part.astype(jnp.bfloat16), "mp").astype(jnp.float32),
        lax.psum(lowrank_piece.astype(jnp.bfloat16), "mp").astype(jnp.float32),
    )
    cot_rows = lax.all_gather(hidden_gradient, "mp", axis=0, tiled=True)
    token_lowrank = low_sum.astype(jnp.bfloat16)
    unscaled_output = base_sum + LOWRANK_SCALE * jnp.einsum(
        "hls,hse->hle", token_lowrank, adapter_up, preferred_element_type=jnp.float32
    )
    gate_proj = unscaled_output[0] * col_ratio[0]
    up_proj = unscaled_output[1] * col_ratio[1]
    activated, derivative = gelu_pair(gate_proj)
    hidden_rows = (activated * up_proj).astype(jnp.bfloat16)
    cotangent = cot_rows.astype(jnp.float32)
    grad_out = jnp.stack([cotangent * up_proj * derivative, cotangent * activated])
    moment_part = jnp.sum(grad_out * unscaled_output, axis=1)
    prescale_gradient = (grad_out * col_ratio[:, None, :]).astype(jnp.bfloat16)
    lowrank_gradient_piece = jnp.einsum(
        "hmu,hmq->huq", token_lowrank, prescale_gradient, preferred_element_type=jnp.float32
    )
    hidden = lax.dynamic_slice_in_dim(hidden_rows, lax.axis_index("mp") * share_rows, share_rows, 0)
    magnitude_gradient = moment_part / col_norm
    frozen_term = -magnitude * moment_part / (col_norm * col_norm * col_norm)
    adapter_up_gradient = LOWRANK_SCALE * (
        lowrank_gradient_piece + mixed_sum * frozen_term[:, None, :]
    )
    lowrank_gradient = jnp.einsum(
        "pge,pbe->pgb", prescale_gradient, adapter_up, preferred_element_type=jnp.float32
    ).astype(jnp.bfloat16)
    weighted_adapter_up = up_broad * frozen_term[:, None, :]
    broadcast_value = jnp.einsum(
        "krf,kdf->krd",
        weighted_adapter_up,
        frozen_weight.astype(jnp.float32),
        precision=MATMUL_ACCURACY,
    )
    inner_gram = jnp.einsum(
        "krf,ksf->krs", weighted_adapter_up, up_broad, precision=MATMUL_ACCURACY
    )
    broadcast_value = broadcast_value + LOWRANK_SCALE * jnp.einsum(
        "krs,ksd->krd", inner_gram, down_broad, precision=MATMUL_ACCURACY
    )
    down_piece = LOWRANK_SCALE * (
        jnp.einsum("ijp,jv->ipv", lowrank_gradient, every_row, preferred_element_type=jnp.float32)
        + broadcast_value
    )
    adapter_down_gradient = lax.psum(down_piece, "dp")
    main_term = jnp.einsum(
        "ktf,kdf->td", prescale_gradient, frozen_weight, preferred_element_type=jnp.float32
    )
    token_gradient = lax.psum_scatter(
        main_term
        + LOWRANK_SCALE
        * jnp.einsum(
            "ijf,ifh->jh", lowrank_gradient, adapter_down, preferred_element_type=jnp.float32
        ),
        "dp",
        scatter_dimension=0,
        tiled=True,
    )
    return (hidden, token_gradient, adapter_down_gradient, adapter_up_gradient, magnitude_gradient)


def solution(mesh):
    in_specs = (
        P("dp", "mp"),
        P(None, "mp", "dp"),
        P(None, None, "mp"),
        P(None, None, "dp"),
        P(None, "dp"),
        P("mp", "dp"),
    )
    out_specs = (
        P("mp", "dp"),
        P("dp", "mp"),
        P(None, None, "mp"),
        P(None, None, "dp"),
        P(None, "dp"),
    )
    return jax.shard_map(
        on_device, mesh=mesh, in_specs=in_specs, out_specs=out_specs, check_vma=False
    )
```

profile of v0, /device:TPU:0, one launch (start us, length us, event | category | flops | bytes accessed | tf_op | source)
XLA Modules:
  0.0 308.0 jit_solution(16763437248531426310)
XLA Ops:
  7.2 0.0 copy-start
  7.2 0.0 all-reduce.9.cloned.1.call-start
  7.2 26.6 %all-gather = bf16[16,12,2304]{2,1,0:T(8,128)(2,1)S(1)} all-gather(bf16[1,12,2304]{2,1,0:T(8,128)(2,1)} %bitcast.66), channel_id=1, replica_groups=mesh['dp'=16,'mp'=2] {'dp'}, dimensions={0}, use_global_device_ids=true | all-gather | bytes 940032 | tf_op jit(solution)/shard_map/all_gather | solution.py:22
  33.9 0.2 reshape.14
  34.1 0.0 copy-start.1
  34.1 12.7 %fusion.2 = bf16[2,192,2304]{2,1,0:T(8,128)(2,1)} fusion(bf16[192,2304,1]{1,0,2:T(8,128)(2,1)S(1)} %reshape.14, bf16[2,2304,2304]{2,1,0:T(8,128)(2,1)} %param.7), kind=kOutput, calls=%fused_computation.4 | convolution fusion | flops 4077748224 | bytes 23887872 | tf_op jit(solution)/shard_map/td,kdf->ktf/dot_general | solution.py:44
  46.8 1.0 copy-done.1
  47.8 3.5 %convolution_convert_fusion.1 = bf16[2,16,2304]{2,1,0:T(8,128)(2,1)} fusion(bf16[2,16,2304]{2,1,0:T(8,128)(2,1)S(1)} %copy-done, bf16[2,2304,2304]{2,1,0:T(8,128)(2,1)S(1)} %copy-done.1), kind=kOutput, calls=%fused_computation.18 | convolution fusion | flops 339812352 | bytes 21528576 | tf_op jit(solution)/shard_map/krd,kdf->krf/dot_general | solution.py:26
  51.3 0.0 all-reduce.9.cloned.1.call-update
  51.3 0.0 all-reduce.7.cloned.1.call-start
  51.4 0.2 convolution_convert_fusion.4
  51.6 0.4 copy-done.8
  52.0 0.6 dynamic-slice.4
  53.2 0.3 fusion.18
  53.6 0.0 copy-start.4
  53.6 0.0 copy-start.2
  53.6 9.3 %multiply_reduce_fusion = bf16[2,2304]{1,0:T(2,128)(2,1)S(1)} fusion(bf16[2,2304,2304]{2,1,0:T(8,128)(2,1)} %param.7), kind=kLoop, calls=%fused_computation | loop fusion | flops 31845888 | bytes 21242880 | tf_op jit(solution)/shard_map/reduce_sum | solution.py:25
  62.9 0.0 copy-start.5
  62.9 9.7 %all-reduce.2 = (bf16[2,192,16]{1,2,0:T(8,128)(2,1)S(1)}, bf16[2,16,16]{2,1,0:T(8,128)(2,1)S(1)}, bf16[2,2304]{1,0:T(2,128)(2,1)S(1)}) all-reduce(bf16[2,192,16]{1,2,0:T(8,128)(2,1)S(1)} %fusion.18, bf16[2,16,16]{2,1,0:T(8,128)(2,1)S(1)} %convolution_convert_fusion.4, ...), channel_id=1, replica_groups=mesh['dp'=16,'mp'=2] {'mp'}, use_global_device_ids=true, to_apply=%region_1.0 | all-reduce | flops 11264 | bytes 45056 | tf_op jit(solution)/shard_map/psum | solution.py:55
  72.7 14.4 %all_gather.7 = bf16[192,2304]{1,0:T(8,128)(2,1)S(1)} all-gather(bf16[96,2304]{1,0:T(8,128)(2,1)S(1)} %copy-done.4), channel_id=1, replica_groups=mesh['dp'=16,'mp'=2] {'mp'}, dimensions={0}, use_global_device_ids=true | all-gather | bytes 1327104 | tf_op jit(solution)/shard_map/all_gather | solution.py:57
  87.1 29.1 %all-reduce.9.cloned.1.call-done = (bf16[2,192,2304]{2,1,0:T(8,128)(2,1)}, bf16[2,16,2304]{2,1,0:T(8,128)(2,1)}) async-done(((bf16[2,192,2304]{2,1,0:T(8,128)(2,1)}, bf16[2,16,2304]{2,1,0:T(8,128)(2,1)}), (bf16[2,192,2304]{2,1,0:T(8,128)(2,1)}, bf16[2,16,2304]{2,1,0:T(8,128)(2,1)})) %all-reduce.9.cloned.1.call-update) | async-done | bytes 1916944 | tf_op jit(solution)/shard_map/psum | solution.py:54
  116.1 1.1 fusion.22
  117.3 0.7 fusion.28
  118.0 2.1 fusion.1
  120.1 3.2 %fusion.10 = (f32[1,192,2304]{2,1,0:T(8,128)S(1)}, f32[192,2304]{1,0:T(8,128)}, f32[1,192,2304]{2,1,0:T(8,128)S(1)}, f32[192,2304]{1,0:T(8,128)}) fusion(bf16[192,2304]{1,0:T(8,128)(2,1)S(1)} %all_gather.7, f32[2304]{0:T(1024)S(1)} %get-tuple-element.7, f32[2,192,2304]{2,1,0:T(8,128)S(1)} %fusion.1, f32[2304]{0:T(1024)S(1)} %get-tuple-element.8), kind=kLoop, calls=%fused_computation.25 | loop fusion | flops 10616832 | bytes 11520000 | tf_op jit(solution)/shard_map/stack | solution.py:67
  123.3 1.1 multiply_reduce_fusion.1
  124.4 11.2 %convolution_bitcast_fusion = f32[192,2304]{1,0:T(8,128)S(1)} fusion(bf16[2,192,2304]{2,1,0:T(8,128)(2,1)S(1)} %get-tuple-element.23, bf16[2,2304,2304]{2,1,0:T(8,128)(2,1)} %param.7), kind=kOutput, calls=%fused_computation.5 | convolution fusion | flops 4076863488 | bytes 24772608 | tf_op jit(solution)/shard_map/ktf,kdf->td/dot_general | solution.py:100
  135.7 0.6 convolution_convert_fusion.2
  136.2 1.7 fusion.4
  137.9 41.5 %fusion = f32[16,2304]{1,0:T(8,128)S(1)} fusion(f32[192,2304]{1,0:T(8,128)} %fusion.4), kind=kCustom, calls=%all-reduce-scatter | all-reduce-scatter fusion | flops 589825 | bytes 1917440
  179.3 0.7 slice.20
  180.0 1.3 collective-permute-start.2
  181.3 2.0 collective-permute-start.1
  183.3 1.9 collective-permute-start
  185.2 0.3 fusion.30
  185.5 1.3 collective-permute-start.3
  186.8 1.4 fusion.29
  188.2 0.3 fusion.20
  188.5 0.3 convolution_multiply_fusion.1
  188.8 20.5 %fusion.7 = f32[2,16,2304]{2,1,0:T(8,128)} fusion(f32[2,16,2304]{2,1,0:T(8,128)S(1)} %fusion.30, f32[2,16,2304]{2,1,0:T(8,128)S(1)} %convolution_multiply_fusion.1, bf16[2,2304,2304]{2,1,0:T(8,128)(2,1)} %param.7, bf16[2,16,2304]{2,1,0:T(8,128)(2,1)S(1)} %copy-done.2, f32[2,2304]{1,0:T(2,128)S(1)} %get-tuple-element.25), kind=kOutput, calls=%fused_computation.17 | convolution fusion | flops 2038800384 | bytes 22284288 | tf_op jit(solution)/shard_map/krf,kdf->krd/dot_general | solution.py:83
  209.3 0.0 all-reduce.7.cloned.1.call-update
  209.4 2.3 fusion.19
  211.7 1.1 fusion.5
  212.8 0.0 collective-permute-done.3
  212.8 2.5 concatenate
  215.3 0.7 constant_dynamic-slice_fusion
  215.9 83.6 %all-reduce.7.cloned.1.call-done = f32[2,16,2304]{2,1,0:T(8,128)} async-done(((f32[2,16,2304]{2,1,0:T(8,128)}), f32[2,16,2304]{2,1,0:T(8,128)}) %all-reduce.7.cloned.1.call-update) | async-done | bytes 294928 | tf_op jit(solution)/shard_map/psum | solution.py:99
  299.5 1.7 copy.14
  (15 shorter events, 0.1 us)
Async XLA Ops:
  7.2 39.6 %copy-start = (bf16[2,16,2304]{2,1,0:T(8,128)(2,1)S(1)}, bf16[2,16,2304]{2,1,0:T(8,128)(2,1)}, u32[]{:S(2)}) copy-start(bf16[2,16,2304]{2,1,0:T(8,128)(2,1)} %param.8) | copy-start | bytes 442372
  7.2 108.9 %all-reduce.9.cloned.1.call-start = ((), (), s32[]{:S(2)}) async-start(), calls=%async_computation.1 | async-start | bytes 3833856 | tf_op jit(solution)/shard_map/psum | solution.py:54
  34.1 13.7 %copy-start.1 = (bf16[2,2304,2304]{2,1,0:T(8,128)(2,1)S(1)}, bf16[2,2304,2304]{2,1,0:T(8,128)(2,1)}, u32[]{:S(2)}) copy-start(bf16[2,2304,2304]{2,1,0:T(8,128)(2,1)} %param.7) | copy-start | bytes 63700996
  51.3 0.7 copy-start.8
  51.3 248.1 %all-reduce.7.cloned.1.call-start = ((), (), s32[]{:S(2)}) async-start(), calls=%async_computation | async-start | bytes 589824 | tf_op jit(solution)/shard_map/psum | solution.py:99
  53.6 19.1 %copy-start.4 = (bf16[96,2304]{1,0:T(8,128)(2,1)S(1)}, bf16[96,2304]{1,0:T(8,128)(2,1)}, u32[]{:S(2)}) copy-start(bf16[96,2304]{1,0:T(8,128)(2,1)} %param.11) | copy-start | bytes 1327108
  53.6 62.5 %copy-start.2 = (bf16[2,16,2304]{2,1,0:T(8,128)(2,1)S(1)}, bf16[2,16,2304]{2,1,0:T(8,128)(2,1)}, u32[]{:S(2)}) copy-start(bf16[2,16,2304]{2,1,0:T(8,128)(2,1)} %param.9) | copy-start | bytes 442372
  62.9 54.4 %copy-start.5 = (f32[2,2304]{1,0:T(2,128)S(1)}, f32[2,2304]{1,0:T(2,128)}, u32[]{:S(2)}) copy-start(f32[2,2304]{1,0:T(2,128)} %param.10) | copy-start | bytes 55300
  72.7 47.4 %copy-start.6 = (bf16[2,192,16]{1,2,0:T(8,128)(2,1)}, bf16[2,192,16]{1,2,0:T(8,128)(2,1)S(1)}, u32[]{:S(2)}) copy-start(bf16[2,192,16]{1,2,0:T(8,128)(2,1)S(1)} %get-tuple-element.9) | copy-start | bytes 36868
  180.0 32.7 %collective-permute-start.2 = (f32[16,2304]{1,0:T(8,128)S(1)}, f32[16,2304]{1,0:T(8,128)S(1)}, u32[]{:S(2)}, u32[]{:S(2)}) collective-permute-start(f32[16,2304]{1,0:T(8,128)S(1)} %fusion), channel_id=1, source_target_pairs={{0,6},{2,8},{4,10},{6,12},{8,14},{10,16},{12,18},{14,20},{16,22},{... | collective-permute-start | bytes 442376
  181.3 31.4 %collective-permute-start.1 = (f32[16,2304]{1,0:T(8,128)S(1)}, f32[16,2304]{1,0:T(8,128)}, u32[]{:S(2)}, u32[]{:S(2)}) collective-permute-start(f32[16,2304]{1,0:T(8,128)S(1)} %fusion), channel_id=1, source_target_pairs={{0,4},{2,6},{4,8},{6,10},{8,12},{10,14},{12,16},{14,18},{16,20},{1... | collective-permute-start | bytes 442376
  183.3 29.5 %collective-permute-start = (f32[16,2304]{1,0:T(8,128)S(1)}, f32[16,2304]{1,0:T(8,128)}, u32[]{:S(2)}, u32[]{:S(2)}) collective-permute-start(f32[16,2304]{1,0:T(8,128)S(1)} %fusion), channel_id=1, source_target_pairs={{0,2},{2,4},{4,6},{6,8},{8,10},{10,12},{12,14},{14,16},{16,18},{18... | collective-permute-start | bytes 442376
  185.5 27.2 %collective-permute-start.3 = (f32[12,2304]{1,0:T(8,128)}, f32[12,2304]{1,0:T(8,128)S(1)}, u32[]{:S(2)}, u32[]{:S(2)}) collective-permute-start(f32[12,2304]{1,0:T(8,128)} %slice.20), channel_id=1, source_target_pairs={{0,8},{2,10},{4,12},{6,14},{8,16},{10,18},{12,20},{14,22},{16,24},... | collective-permute-start | bytes 331784
  209.3 2.4 copy-start.3
  209.3 2.4 copy-start.7
Sparse Core Ops, SparseCore 0:
  51.5 64.5 all-reduce.8
  209.5 89.9 all-reduce.6
where the time goes:
time: 309 us; the launch traced here: 308 us
  waiting for transfers between devices  113 us (37%)
  blocking collectives  92.2 us (30%)
  matrix products  55.8 us (18%)
  other arithmetic  18 us (6%)
  between operations  14.9 us (5%)
  local copies, waits for them, and re-layouts  7.86 us (3%)
  starting transfers between devices  6.56 us (2%)
    psum x1, waiting for transfers between devices, on_device(): adapter_down_gradient = lax.psum(down_piece, 'dp')  83.6 us
    unnamed x1, blocking collectives  41.5 us
    psum x1, waiting for transfers between devices, on_device(): lax.psum(base_part.astype(jnp.bfloat16), 'mp').astype(jnp.float32)  29.1 us
    all_gather x1, blocking collectives, on_device(): every_row = lax.all_gather(tokens, 'dp', axis=0, tiled=True)  26.6 us
    dot_general x1, matrix products, on_device(): jnp.einsum('krf,kdf->krd', weighted_adapter_up, frozen_weight.astype(jnp....  20.5 us
    all_gather x1, blocking collectives, on_device(): cot_rows = lax.all_gather(hidden_gradient, 'mp', axis=0, tiled=True)  14.4 us
    dot_general x1, matrix products, on_device(): jnp.einsum('td,kdf->ktf', every_row, frozen_weight, preferred_element_typ...  12.7 us
    dot_general x1, matrix products, on_device(): jnp.einsum('ktf,kdf->td', prescale_gradient, frozen_weight, preferred_ele...  11.2 us
  transfers between devices with their start and end apart: 6, of which 2 were waited for; matrix products, arithmetic and copies ran while one was open for 13% of the time, Pallas kernels for 0%

commit v1 on v0

--- a/solution.py
+++ b/solution.py
@@ -1,6 +1,10 @@
+import functools
+
 import jax
 import jax.numpy as jnp
 from jax import lax
+from jax.experimental import pallas as pl
+from jax.experimental.pallas import tpu as pltpu
 from jax.sharding import PartitionSpec as P
 
 LOWRANK_SCALE = 2.0
@@ -113,6 +117,368 @@
     return (hidden, token_gradient, adapter_down_gradient, adapter_up_gradient, magnitude_gradient)
 
 
+MESH = pl.DeviceIdType.MESH
+TILE = 256
+LANES = 128
+BLOCK = 16
+
+
+def mm(left, right, precision=None):
+    return lax.dot_general(
+        left, right, (((1,), (0,)), ((), ())), precision=precision, preferred_element_type=jnp.float32
+    )
+
+
+def nt(left, right):
+    return lax.dot_general(left, right, (((1,), (1,)), ((), ())), preferred_element_type=jnp.float32)
+
+
+def fused_kernel(
+    n_dp, chunks,
+    tok, w, ad, up, mag, cot, gather_map, scatter_map,
+    hid, tgrad, agrad, ugrad, mgrad,
+    wv, tokpad, toks, mx_s, mx_r, sq_s, sq_r, tl_s, tl_r, tl_sum,
+    base_s, base_o, base_r, gp, gr, mo, mr, lhs, tacc, aacc, glow, igram,
+    blk, rsb, asum, agb,
+    wsem, ag_ss, ag_rs, y_ss, y_rs, rs_ss, rs_rs, ah_ss, ah_rs,
+):
+    f32, bf16 = jnp.float32, jnp.bfloat16
+    me = lax.axis_index("dp")
+    mate = 1 - lax.axis_index("mp")
+    rows, depth, width = tok.shape[0], w.shape[1], w.shape[2]
+    rank = ad.shape[1]
+    half = cot.shape[0]
+    cw = width // chunks
+    t = tgrad.shape[0]
+    share = agrad.shape[1]
+
+    loads = {}
+    for c in range(chunks):
+        for k in range(2):
+            cut = pl.ds(c * cw, cw)
+            copy = pltpu.make_async_copy(w.at[k, :, cut], wv.at[k, :, cut], wsem.at[c, k])
+            copy.start()
+            loads[c, k] = copy
+
+    barrier = pltpu.get_barrier_semaphore()
+    for i in range(1, n_dp):
+        pl.semaphore_signal(barrier, inc=1, device_id={"dp": lax.rem(me + i, n_dp)}, device_id_type=MESH)
+    pl.semaphore_signal(barrier, inc=1, device_id={"mp": mate}, device_id_type=MESH)
+    pl.semaphore_wait(barrier, n_dp)
+
+    def to_dp(source, target, ss, rs, i):
+        return pltpu.make_async_remote_copy(
+            src_ref=source, dst_ref=target, send_sem=ss.at[i], recv_sem=rs.at[i],
+            device_id={"dp": lax.rem(me + i, n_dp)}, device_id_type=MESH,
+        )
+
+    used = []
+
+    def to_mate(source, target):
+        i = len(used)
+        copy = pltpu.make_async_remote_copy(
+            src_ref=source, dst_ref=target, send_sem=y_ss.at[i], recv_sem=y_rs.at[i],
+            device_id={"mp": mate}, device_id_type=MESH,
+        )
+        used.append(copy)
+        copy.start()
+        return copy
+
+    gathers = []
+    for i in range(1, n_dp):
+        copy = to_dp(tok, tokpad.at[me], ag_ss, ag_rs, i)
+        copy.start()
+        gathers.append(copy)
+    tokpad[me] = tok[...]
+
+    stats = []
+    for c in range(chunks):
+        for k in range(2):
+            loads[c, k].wait()
+            cols = pl.ds(c * cw, cw)
+
+            def stat_step(r, carry):
+                cross, square = carry
+                at = pl.ds(pl.multiple_of(r * TILE, TILE), TILE)
+                piece = wv[k, at, cols]
+                wide = piece.astype(f32)
+                cross = cross + mm(ad[k, :, at], piece)
+                square = square + jnp.sum((wide * wide).reshape(TILE // 8, 8, cw), axis=0)
+                return cross, square
+
+            cross, square = lax.fori_loop(
+                0, depth // TILE, stat_step, (jnp.zeros((rank, cw), f32), jnp.zeros((8, cw), f32))
+            )
+            gram = nt(ad[k], ad[k])
+            up32 = up[k, :, cols].astype(f32)
+            gram_up = mm(gram, up32, MATMUL_ACCURACY)
+            total = (
+                jnp.sum(square, axis=0, keepdims=True)
+                + 2.0 * LOWRANK_SCALE * jnp.sum(up32 * cross, axis=0, keepdims=True)
+                + LOWRANK_SCALE * LOWRANK_SCALE * jnp.sum(up32 * gram_up, axis=0, keepdims=True)
+            )
+            mx_s[c, k * rank : (k + 1) * rank, :] = (cross + LOWRANK_SCALE * gram_up).astype(bf16)
+            sq_s[c, k : k + 1, :] = total
+        stats.append((to_mate(mx_s.at[c], mx_r.at[c]), to_mate(sq_s.at[c], sq_r.at[c])))
+
+    for copy in gathers:
+        copy.wait()
+
+    def gather_step(r, carry):
+        at = pl.ds(pl.multiple_of(r * TILE, TILE), TILE)
+        piece = tokpad[:, :, at].reshape(n_dp * BLOCK, TILE)
+        toks[:, at] = mm(gather_map[...], piece).astype(bf16)
+        return carry
+
+    lax.fori_loop(0, depth // TILE, gather_step, 0)
+
+    for k in range(2):
+        low = nt(toks[...], ad[k]).astype(bf16)
+        tl_s[0, k] = low[:half]
+        tl_s[1, k] = low[half:]
+    low_copy = to_mate(tl_s, tl_r)
+
+    base_copies = []
+    for c in range(chunks):
+
+        def base_step(j, carry):
+            at = pl.ds(pl.multiple_of(j * TILE, TILE), TILE)
+            for k in range(2):
+                piece = wv[k, :, pl.ds(pl.multiple_of(c * cw + j * TILE, TILE), TILE)]
+                part = mm(toks[...], piece).astype(bf16)
+                base_s[c, k, :, at] = part[:half]
+                base_o[c, k, :, at] = part[half:]
+            return carry
+
+        lax.fori_loop(0, cw // TILE, base_step, 0)
+        base_copies.append(to_mate(base_s.at[c], base_r.at[c]))
+
+    low_copy.wait()
+    for k in range(2):
+        tl_sum[0, k] = (tl_s[0, k].astype(f32) + tl_r[1, k].astype(f32)).astype(bf16)
+        tl_sum[1, k] = (tl_s[1, k].astype(f32) + tl_r[0, k].astype(f32)).astype(bf16)
+
+    grads = []
+    for c in range(chunks):
+        for copy in stats[c]:
+            copy.wait()
+        base_copies[c].wait()
+
+        def point_step(j, carry):
+            at = pl.ds(pl.multiple_of(j * LANES, LANES), LANES)
+            wide_at = pl.ds(pl.multiple_of(c * cw + j * LANES, LANES), LANES)
+            pres, ratios = [], []
+            for k in range(2):
+                norm = jnp.sqrt(sq_s[c, k : k + 1, at] + sq_r[c, k : k + 1, at] + EPSILON)
+                ratios.append(mag[k : k + 1, wide_at] / norm)
+                base = base_o[c, k, :, at].astype(f32) + base_r[c, k, :, at].astype(f32)
+                pres.append(base + LOWRANK_SCALE * mm(tl_sum[1, k], up[k, :, wide_at]))
+            gate, upper = pres[0] * ratios[0], pres[1] * ratios[1]
+            activated, derivative = gelu_pair(gate)
+            hid[:, wide_at] = (activated * upper).astype(bf16)
+            cotangent = cot[:, wide_at].astype(f32)
+            outs = (cotangent * upper * derivative, cotangent * activated)
+            for k in range(2):
+                mo[c, k : k + 1, at] = jnp.sum(outs[k] * pres[k], axis=0, keepdims=True)
+                gp[c, k, :, at] = (outs[k] * ratios[k]).astype(bf16)
+            return carry
+
+        lax.fori_loop(0, cw // LANES, point_step, 0)
+        grads.append((to_mate(gp.at[c], gr.at[c]), to_mate(mo.at[c], mr.at[c])))
+
+    for c in range(chunks):
+        for copy in grads[c]:
+            copy.wait()
+        cols = pl.ds(c * cw, cw)
+        for k in range(2):
+            moment = mo[c, k : k + 1, :] + mr[c, k : k + 1, :]
+            norm = jnp.sqrt(sq_s[c, k : k + 1, :] + sq_r[c, k : k + 1, :] + EPSILON)
+            mgrad[k : k + 1, cols] = moment / norm
+            frozen_term = -mag[k : k + 1, cols] * moment / (norm * norm * norm)
+            part = pl.ds(k * rank, rank)
+            mixed = mx_s[c, part, :].astype(f32) + mx_r[c, part, :].astype(f32)
+            up16 = up[k, :, cols]
+            weighted = up16.astype(f32) * frozen_term
+            high = weighted.astype(bf16)
+            low = (weighted - high.astype(f32)).astype(bf16)
+            theirs, mine = gr[c, k], gp[c, k]
+            piece = mm(tl_sum[0, k].astype(f32).T.astype(bf16), theirs) + mm(
+                tl_sum[1, k].astype(f32).T.astype(bf16), mine
+            )
+            ugrad[k, :, cols] = LOWRANK_SCALE * (piece + mixed * frozen_term)
+            lhs[k, 0:half, :] = theirs
+            lhs[k, half : 2 * half, :] = mine
+            lhs[k, 2 * half : 2 * half + rank, :] = high
+            lhs[k, 2 * half + rank : 2 * half + 2 * rank, :] = low
+            small = nt(lhs[k], up16)
+            gl, ig = small[: 2 * half], small[2 * half : 2 * half + rank] + small[2 * half + rank :]
+            if c == 0:
+                glow[k] = gl
+                igram[k] = ig
+            else:
+                glow[k] += gl
+                igram[k] += ig
+
+        def grad_step(r, carry):
+            at = pl.ds(pl.multiple_of(r * TILE, TILE), TILE)
+            outs = [nt(lhs[k], wv[k, at, cols]) for k in range(2)]
+            main = outs[0][: 2 * half] + outs[1][: 2 * half]
+            if c == 0:
+                tacc[:, at] = main
+            else:
+                tacc[:, at] += main
+            for k in range(2):
+                spread = outs[k][2 * half : 2 * half + rank] + outs[k][2 * half + rank :]
+                if c == 0:
+                    aacc[k, :, at] = spread
+                else:
+                    aacc[k, :, at] += spread
+            return carry
+
+        lax.fori_loop(0, depth // TILE, grad_step, 0)
+
+    def final_step(r, carry):
+        at = pl.ds(pl.multiple_of(r * TILE, TILE), TILE)
+        main = tacc[:, at]
+        parts = []
+        for k in range(2):
+            low = glow[k].astype(bf16)
+            adt = ad[k, :, at]
+            main = main + LOWRANK_SCALE * mm(low, adt)
+            spread = aacc[k, :, at] + LOWRANK_SCALE * mm(igram[k], adt.astype(f32), MATMUL_ACCURACY)
+            parts.append(LOWRANK_SCALE * (mm(glow[k].T.astype(bf16), toks[:, at]) + spread))
+        whole = jnp.concatenate([main] + parts, axis=0).astype(bf16)
+        packed = mm(scatter_map[...], whole).astype(bf16)
+        blk[:, :, at] = packed.reshape(n_dp, BLOCK, TILE)
+        return carry
+
+    lax.fori_loop(0, depth // TILE, final_step, 0)
+
+    scatters = []
+    for i in range(1, n_dp):
+        copy = to_dp(blk.at[lax.rem(me + i, n_dp)], rsb.at[i], rs_ss, rs_rs, i)
+        copy.start()
+        scatters.append(copy)
+    rsb[0] = blk[me]
+    for copy in scatters:
+        copy.wait()
+
+    def sum_step(r, carry):
+        at = pl.ds(pl.multiple_of(r * TILE, TILE), TILE)
+        total = rsb[0, :, at].astype(f32)
+        for i in range(1, n_dp):
+            total = total + rsb[i, :, at].astype(f32)
+        tgrad[:, at] = total[:t]
+        asum[:, at] = total[t : t + share]
+        return carry
+
+    lax.fori_loop(0, depth // TILE, sum_step, 0)
+
+    spreads = []
+    for i in range(1, n_dp):
+        copy = to_dp(asum, agb.at[me], ah_ss, ah_rs, i)
+        copy.start()
+        spreads.append(copy)
+    agb[me] = asum[...]
+    for copy in spreads:
+        copy.wait()
+    agrad[...] = agb[...]
+
+
+def fused_on_device(n_dp, chunks, tokens, frozen_weight, adapter_down, adapter_up, magnitude, hidden_gradient):
+    f32, bf16 = jnp.float32, jnp.bfloat16
+    t, depth = tokens.shape
+    rank, width = adapter_up.shape[1:]
+    half = hidden_gradient.shape[0]
+    count = n_dp * t
+    share = 2 * rank // n_dp
+    cw = width // chunks
+    first = (1 - lax.axis_index("mp")) * half
+    order = (jnp.arange(count) + first) % count
+    places = (order // t) * BLOCK + order % t
+    slots = jnp.arange(n_dp * BLOCK)
+    gather_map = (places[:, None] == slots[None, :]).astype(bf16)
+    spots = jnp.arange(2 * rank)
+    spots = (spots // share) * BLOCK + t + spots % share
+    scatter_map = (slots[:, None] == jnp.concatenate([places, spots])[None, :]).astype(bf16)
+    padded = jnp.pad(tokens, ((0, BLOCK - t), (0, 0)))
+    vmem = pl.BlockSpec(memory_space=pltpu.VMEM)
+    dma = pltpu.SemaphoreType.DMA
+    V = pltpu.VMEM
+    messages = 5 * chunks + 1 + chunks
+    hidden, tgrad, agrad, ugrad, mgrad = pl.pallas_call(
+        functools.partial(fused_kernel, n_dp, chunks),
+        out_shape=(
+            jax.ShapeDtypeStruct((half, width), bf16),
+            jax.ShapeDtypeStruct((t, depth), f32),
+            jax.ShapeDtypeStruct((n_dp, share, depth), f32),
+            jax.ShapeDtypeStruct((2, rank, width), f32),
+            jax.ShapeDtypeStruct((2, width), f32),
+        ),
+        in_specs=[vmem, pl.BlockSpec(memory_space=pl.ANY)] + [vmem] * 6,
+        out_specs=(vmem,) * 5,
+        scratch_shapes=[
+            V((2, depth, width), bf16),
+            V((n_dp, BLOCK, depth), bf16),
+            V((count, depth), bf16),
+            V((chunks, 2 * rank, cw), bf16),
+            V((chunks, 2 * rank, cw), bf16),
+            V((chunks, 2, cw), f32),
+            V((chunks, 2, cw), f32),
+            V((2, 2, half, rank), bf16),
+            V((2, 2, half, rank), bf16),
+            V((2, 2, half, rank), bf16),
+            V((chunks, 2, half, cw), bf16),
+            V((chunks, 2, half, cw), bf16),
+            V((chunks, 2, half, cw), bf16),
+            V((chunks, 2, half, cw), bf16),
+            V((chunks, 2, half, cw), bf16),
+            V((chunks, 2, cw), f32),
+            V((chunks, 2, cw), f32),
+            V((2, count + 2 * rank, cw), bf16),
+            V((count, depth), f32),
+            V((2, rank, depth), f32),
+            V((2, count, rank), f32),
+            V((2, rank, rank), f32),
+            V((n_dp, BLOCK, depth), bf16),
+            V((n_dp, BLOCK, depth), bf16),
+            V((share, depth), f32),
+            V((n_dp, share, depth), f32),
+            dma((chunks, 2)),
+            dma((n_dp,)), dma((n_dp,)),
+            dma((messages,)), dma((messages,)),
+            dma((n_dp,)), dma((n_dp,)),
+            dma((n_dp,)), dma((n_dp,)),
+        ],
+        compiler_params=pltpu.CompilerParams(
+            collective_id=0, has_side_effects=True, vmem_limit_bytes=64_000_000
+        ),
+        name="dora_pair",
+    )(padded, frozen_weight, adapter_down, adapter_up, magnitude, hidden_gradient, gather_map, scatter_map)
+    return hidden, tgrad, agrad.reshape(2, rank, depth), ugrad, mgrad
+
+
+def per_device(n_dp, n_mp, *arrays):
+    tokens, frozen_weight, _, adapter_up, _, hidden_gradient = arrays
+    t, depth = tokens.shape
+    rank, width = adapter_up.shape[1:]
+    fits = (
+        n_mp == 2
+        and depth % TILE == 0
+        and width % (CHUNKS * TILE) == 0
+        and (2 * rank) % n_dp == 0
+        and t + 2 * rank // n_dp <= BLOCK
+        and hidden_gradient.shape[0] % 16 == 0
+        and 2 * frozen_weight.size <= 24 * 2**20
+    )
+    if fits:
+        return fused_on_device(n_dp, CHUNKS, *arrays)
+    return on_device(*arrays)
+
+
+CHUNKS = 3
+
+
 def solution(mesh):
     in_specs = (
         P("dp", "mp"),
@@ -130,5 +496,5 @@
         P(None, "dp"),
     )
     return jax.shard_map(
-        on_device, mesh=mesh, in_specs=in_specs, out_specs=out_specs, check_vma=False
-    )
+        functools.partial(per_device, mesh.shape["dp"], mesh.shape["mp"]), mesh=mesh, in_specs=in_specs, out_specs=out_specs, check_vma=False
+    )

time: 309 us -> 137 us (0.44)
  Pallas kernels: 0 us -> 124 us
  waiting for transfers between devices: 113 us -> 0 us
  blocking collectives: 92.2 us -> 0 us
  matrix products: 55.8 us -> 0 us
  other arithmetic: 18 us -> 1.53 us
  between operations: 14.9 us -> 0.65 us
  starting transfers between devices: 6.56 us -> 0 us
    pallas_call x0 -> x1, Pallas kernels: none -> 124 us  [fused_on_device(): pl.pallas_call(functools.partial(fused_kernel, n_dp, chunks), out_shape=(...]
    psum x2 -> x0, waiting for transfers between devices: 113 us -> none  [the longest x1 83.6 us: on_device(): adapter_down_gradient = lax.psum(down_piece, 'dp')]
    dot_general x14 -> x0, matrix products: 55.8 us -> none  [the longest x1 20.5 us: on_device(): jnp.einsum('krf,kdf->krd', weighted_adapter_up, frozen_weight.astype(jnp....]
    unnamed x1 -> x0, blocking collectives: 41.5 us -> none
    all_gather x2 -> x0, blocking collectives: 41 us -> none  [the longest x1 26.6 us: on_device(): every_row = lax.all_gather(tokens, 'dp', axis=0, tiled=True)]
    reduce_sum x2 -> x0, other arithmetic: 10.4 us -> none  [the longest x1 9.28 us: on_device(): base_square = jnp.sum(jnp.square(frozen_weight.astype(jnp.float32)), axis=1)]
    psum x1 -> x0, blocking collectives: 9.73 us -> none  [on_device(): lax.psum(lowrank_piece.astype(jnp.bfloat16), 'mp').astype(jnp.float32)]
    unnamed x4 -> x0, starting transfers between devices: 6.48 us -> none
  transfers between devices with their start and end apart: 6 -> 0, of which waited for: 2 -> 0; matrix products, arithmetic and copies ran while one was open for 13% -> 0% of each run, Pallas kernels for 0% -> 0%
where the time goes in v1:
time: 137 us; the launch traced here: 136 us
  Pallas kernels  124 us (91%)
  local copies, waits for them, and re-layouts  9.81 us (7%)
  other arithmetic  1.53 us (1%)
    pallas_call x1, Pallas kernels, fused_on_device(): pl.pallas_call(functools.partial(fused_kernel, n_dp, chunks), out_shape=(...  124 us
    unnamed x4, local copies, waits for them, and re-layouts  6.4 us

profile of v1, /device:TPU:0, one launch (start us, length us, event | category | flops | bytes accessed | tf_op | source)
XLA Modules:
  0.0 136.3 jit_solution(15932739017544973291)
XLA Ops:
  0.7 0.1 pad_add_fusion
  0.8 1.5 %pad.4.tok = bf16[16,2304]{1,0:T(8,128)(2,1)} pad(bf16[12,2304]{1,0:T(8,128)(2,1)} %param.6, bf16[]{:T(256)} %constant.58.clone.1), padding=0_4x0_0 | pad | bytes 129026 | tf_op jit(solution)/shard_map/jit(_pad)/pad | solution.py:404
  2.3 0.7 fusion.1.gather_map
  3.0 0.7 fusion.scatter_map
  3.7 124.3 %dora_pair.1 = (bf16[96,2304]{1,0:T(8,128)(2,1)}, f32[12,2304]{1,0:T(8,128)}, f32[16,2,2304]{2,1,0:T(2,128)}, f32[2,16,2304]{2,1,0:T(8,128)}, f32[2,2304]{1,0:T(2,128)}) custom-call(bf16[16,2304]{1,0:T(8,128)(2,1)} %pad.4.tok, bf16[2,2304,2304]{2,1,0:T(8,128)(2,1)} %w.1, bf16[2,16,2304]{2,1,0:T(8,128)(2,1)} %ad.1, bf16[2,16,2304]{2,1,0:T(8,128)(2,1)} %up.1, ...), custom_call_target="tpu_custom_call" | custom-call | tf_op jit(solution)/shard_map/dora_pair/pallas_call | solution.py:409
  128.0 1.9 %reshape.38 = f32[2,16,2304]{2,1,0:T(8,128)} reshape(f32[16,2,2304]{2,1,0:T(2,128)} %get-tuple-element.12) | data formatting | bytes 589824 | tf_op jit(solution)/shard_map/reshape | solution.py:458
  129.9 1.8 %copy.15 = bf16[96,2304]{1,0:T(8,128)(2,1)} copy(bf16[96,2304]{1,0:T(8,128)(2,1)} %get-tuple-element.20) | data formatting | bytes 884736
  131.7 1.6 %copy.16 = f32[12,2304]{1,0:T(8,128)} copy(f32[12,2304]{1,0:T(8,128)} %get-tuple-element.21) | data formatting | bytes 221184
  133.3 1.7 %copy.17 = f32[2,16,2304]{2,1,0:T(8,128)} copy(f32[2,16,2304]{2,1,0:T(8,128)} %get-tuple-element.23) | data formatting | bytes 589824
  135.0 1.3 copy.18
  (2 shorter events, 0.0 us)

commit v2 on v1

--- a/solution.py
+++ b/solution.py
@@ -2,6 +2,7 @@
 
 import jax
 import jax.numpy as jnp
+import numpy as np
 from jax import lax
 from jax.experimental import pallas as pl
 from jax.experimental.pallas import tpu as pltpu
@@ -137,20 +138,21 @@
     n_dp, chunks,
     tok, w, ad, up, mag, cot, gather_map, scatter_map,
     hid, tgrad, agrad, ugrad, mgrad,
-    wv, tokpad, toks, mx_s, mx_r, sq_s, sq_r, tl_s, tl_r, tl_sum,
+    wv, sent, tokpad, toks, mx_s, mx_r, sq_s, sq_r, tl_s, tl_r, tl_sum,
     base_s, base_o, base_r, gp, gr, mo, mr, lhs, tacc, aacc, glow, igram,
-    blk, rsb, asum, agb,
-    wsem, ag_ss, ag_rs, y_ss, y_rs, rs_ss, rs_rs, ah_ss, ah_rs,
+    blk, prb, own, rsb, asum, agb,
+    wsem, pr_ss, pr_rs, ag_ss, ag_rs, y_ss, y_rs, rs_ss, rs_rs, ah_ss, ah_rs,
 ):
     f32, bf16 = jnp.float32, jnp.bfloat16
     me = lax.axis_index("dp")
     mate = 1 - lax.axis_index("mp")
-    rows, depth, width = tok.shape[0], w.shape[1], w.shape[2]
+    depth, width = w.shape[1], w.shape[2]
     rank = ad.shape[1]
     half = cot.shape[0]
     cw = width // chunks
     t = tgrad.shape[0]
-    share = agrad.shape[1]
+    share = asum.shape[0]
+    side = lax.axis_index("mp")
 
     loads = {}
     for c in range(chunks):
@@ -160,17 +162,43 @@
             copy.start()
             loads[c, k] = copy
 
+    sent[...] = jnp.concatenate([tok[...], jnp.zeros((BLOCK - t, depth), bf16)], axis=0)
+
     barrier = pltpu.get_barrier_semaphore()
     for i in range(1, n_dp):
         pl.semaphore_signal(barrier, inc=1, device_id={"dp": lax.rem(me + i, n_dp)}, device_id_type=MESH)
     pl.semaphore_signal(barrier, inc=1, device_id={"mp": mate}, device_id_type=MESH)
     pl.semaphore_wait(barrier, n_dp)
 
-    def to_dp(source, target, ss, rs, i):
-        return pltpu.make_async_remote_copy(
+    chips = n_dp // 2
+    chip, core = me // 2, lax.rem(me, 2)
+    partner = 2 * chip + 1 - core
+
+    def to_dp(source, target, ss, rs, i, peer):
+        copy = pltpu.make_async_remote_copy(
             src_ref=source, dst_ref=target, send_sem=ss.at[i], recv_sem=rs.at[i],
-            device_id={"dp": lax.rem(me + i, n_dp)}, device_id_type=MESH,
+            device_id={"dp": peer}, device_id_type=MESH,
         )
+        copy.start()
+        return copy
+
+    def gather_start(source, target, ss, rs):
+        copies = [to_dp(source, target.at[me], ss, rs, 0, partner)]
+        for i in range(1, chips):
+            peer = lax.rem(me + 2 * i, n_dp)
+            copies.append(to_dp(source, target.at[me], ss, rs, i, peer))
+        target[me] = source[...]
+        return copies
+
+    def gather_finish(copies, target, ss, rs):
+        relays = []
+        for i in range(1, chips):
+            copies[i].wait()
+            came = lax.rem(me + n_dp - 2 * i, n_dp)
+            relays.append(to_dp(target.at[came], target.at[came], ss, rs, chips + i, partner))
+        copies[0].wait()
+        for copy in relays:
+            copy.wait()
 
     used = []
 
@@ -184,12 +212,7 @@
         copy.start()
         return copy
 
-    gathers = []
-    for i in range(1, n_dp):
-        copy = to_dp(tok, tokpad.at[me], ag_ss, ag_rs, i)
-        copy.start()
-        gathers.append(copy)
-    tokpad[me] = tok[...]
+    gathers = gather_start(sent, tokpad, ag_ss, ag_rs)
 
     stats = []
     for c in range(chunks):
@@ -221,13 +244,12 @@
             sq_s[c, k : k + 1, :] = total
         stats.append((to_mate(mx_s.at[c], mx_r.at[c]), to_mate(sq_s.at[c], sq_r.at[c])))
 
-    for copy in gathers:
-        copy.wait()
+    gather_finish(gathers, tokpad, ag_ss, ag_rs)
 
     def gather_step(r, carry):
         at = pl.ds(pl.multiple_of(r * TILE, TILE), TILE)
         piece = tokpad[:, :, at].reshape(n_dp * BLOCK, TILE)
-        toks[:, at] = mm(gather_map[...], piece).astype(bf16)
+        toks[:, at] = mm(gather_map[side], piece).astype(bf16)
         return carry
 
     lax.fori_loop(0, depth // TILE, gather_step, 0)
@@ -348,41 +370,63 @@
             spread = aacc[k, :, at] + LOWRANK_SCALE * mm(igram[k], adt.astype(f32), MATMUL_ACCURACY)
             parts.append(LOWRANK_SCALE * (mm(glow[k].T.astype(bf16), toks[:, at]) + spread))
         whole = jnp.concatenate([main] + parts, axis=0).astype(bf16)
-        packed = mm(scatter_map[...], whole).astype(bf16)
+        packed = mm(scatter_map[side], whole).astype(bf16)
         blk[:, :, at] = packed.reshape(n_dp, BLOCK, TILE)
         return carry
 
-    lax.fori_loop(0, depth // TILE, final_step, 0)
+    tiles = depth // TILE // CUTS
+    pairs = []
+    for q in range(CUTS):
+        lax.fori_loop(q * tiles, (q + 1) * tiles, final_step, 0)
+        cut = pl.ds(q * tiles * TILE, tiles * TILE)
+        pairs.append(to_dp(blk.at[pl.ds((1 - core) * chips, chips), :, cut], prb.at[:, :, cut], pr_ss, pr_rs, q, partner))
 
     scatters = []
-    for i in range(1, n_dp):
-        copy = to_dp(blk.at[lax.rem(me + i, n_dp)], rsb.at[i], rs_ss, rs_rs, i)
-        copy.start()
-        scatters.append(copy)
-    rsb[0] = blk[me]
-    for copy in scatters:
-        copy.wait()
-
-    def sum_step(r, carry):
-        at = pl.ds(pl.multiple_of(r * TILE, TILE), TILE)
-        total = rsb[0, :, at].astype(f32)
-        for i in range(1, n_dp):
-            total = total + rsb[i, :, at].astype(f32)
-        tgrad[:, at] = total[:t]
-        asum[:, at] = total[t : t + share]
-        return carry
-
-    lax.fori_loop(0, depth // TILE, sum_step, 0)
-
-    spreads = []
-    for i in range(1, n_dp):
-        copy = to_dp(asum, agb.at[me], ah_ss, ah_rs, i)
-        copy.start()
-        spreads.append(copy)
-    agb[me] = asum[...]
-    for copy in spreads:
-        copy.wait()
-    agrad[...] = agb[...]
+    for q in range(CUTS):
+        pairs[q].wait()
+
+        def pair_step(r, carry):
+            at = pl.ds(pl.multiple_of(r * TILE, TILE), TILE)
+            for j in range(chips):
+                total = blk[core * chips + j, :, at].astype(f32) + prb[j, :, at].astype(f32)
+                own[j, :, at] = total.astype(bf16)
+            return carry
+
+        lax.fori_loop(q * tiles, (q + 1) * tiles, pair_step, 0)
+        cut = pl.ds(q * tiles * TILE, tiles * TILE)
+        sends = []
+        for i in range(1, chips):
+            there = lax.rem(chip + i, chips)
+            sends.append(
+                to_dp(own.at[there, :, cut], rsb.at[i, :, cut], rs_ss, rs_rs, q * chips + i, 2 * there + core)
+            )
+        scatters.append(sends)
+
+    for q in range(CUTS):
+        for copy in scatters[q]:
+            copy.wait()
+
+        def sum_step(r, carry):
+            at = pl.ds(pl.multiple_of(r * TILE, TILE), TILE)
+            total = own[chip, :, at].astype(f32)
+            for i in range(1, chips):
+                total = total + rsb[i, :, at].astype(f32)
+            tgrad[:, at] = total[:t]
+            asum[:, at] = total[t : t + share].astype(bf16)
+            return carry
+
+        lax.fori_loop(q * tiles, (q + 1) * tiles, sum_step, 0)
+
+    spreads = gather_start(asum, agb, ah_ss, ah_rs)
+    gather_finish(spreads, agb, ah_ss, ah_rs)
+    for b in range(n_dp):
+        k, row = (b * share) // rank, (b * share) % rank
+        agrad[k, row : row + share, :] = agb[b].astype(f32)
+
+
+def copy_kernel(*refs):
+    for source, target in zip(refs[:5], refs[5:]):
+        target[...] = source[...]
 
 
 def fused_on_device(n_dp, chunks, tokens, frozen_weight, adapter_down, adapter_up, magnitude, hidden_gradient):
@@ -393,32 +437,38 @@
     count = n_dp * t
     share = 2 * rank // n_dp
     cw = width // chunks
-    first = (1 - lax.axis_index("mp")) * half
-    order = (jnp.arange(count) + first) % count
-    places = (order // t) * BLOCK + order % t
-    slots = jnp.arange(n_dp * BLOCK)
-    gather_map = (places[:, None] == slots[None, :]).astype(bf16)
-    spots = jnp.arange(2 * rank)
-    spots = (spots // share) * BLOCK + t + spots % share
-    scatter_map = (slots[:, None] == jnp.concatenate([places, spots])[None, :]).astype(bf16)
-    padded = jnp.pad(tokens, ((0, BLOCK - t), (0, 0)))
+    slots = np.arange(n_dp * BLOCK)
+    by_core = lambda block: (block % 2) * (n_dp // 2) + block // 2
+    spots = np.arange(2 * rank)
+    spots = by_core(spots // share) * BLOCK + t + spots % share
+    gathers, scatters = [], []
+    for side in range(2):
+        order = (np.arange(count) + (1 - side) * half) % count
+        places = (order // t) * BLOCK + order % t
+        homes = by_core(order // t) * BLOCK + order % t
+        gathers.append(places[:, None] == slots[None, :])
+        scatters.append(slots[:, None] == np.concatenate([homes, spots])[None, :])
+    gather_map = jnp.asarray(np.stack(gathers), bf16)
+    scatter_map = jnp.asarray(np.stack(scatters), bf16)
     vmem = pl.BlockSpec(memory_space=pltpu.VMEM)
     dma = pltpu.SemaphoreType.DMA
     V = pltpu.VMEM
     messages = 5 * chunks + 1 + chunks
-    hidden, tgrad, agrad, ugrad, mgrad = pl.pallas_call(
+    shapes = (
+        jax.ShapeDtypeStruct((half, width), bf16),
+        jax.ShapeDtypeStruct((t, depth), f32),
+        jax.ShapeDtypeStruct((2, rank, depth), f32),
+        jax.ShapeDtypeStruct((2, rank, width), f32),
+        jax.ShapeDtypeStruct((2, width), f32),
+    )
+    outs = pl.pallas_call(
         functools.partial(fused_kernel, n_dp, chunks),
-        out_shape=(
-            jax.ShapeDtypeStruct((half, width), bf16),
-            jax.ShapeDtypeStruct((t, depth), f32),
-            jax.ShapeDtypeStruct((n_dp, share, depth), f32),
-            jax.ShapeDtypeStruct((2, rank, width), f32),
-            jax.ShapeDtypeStruct((2, width), f32),
-        ),
+        out_shape=shapes,
         in_specs=[vmem, pl.BlockSpec(memory_space=pl.ANY)] + [vmem] * 6,
         out_specs=(vmem,) * 5,
         scratch_shapes=[
             V((2, depth, width), bf16),
+            V((BLOCK, depth), bf16),
             V((n_dp, BLOCK, depth), bf16),
             V((count, depth), bf16),
             V((chunks, 2 * rank, cw), bf16),
@@ -441,21 +491,26 @@
             V((2, count, rank), f32),
             V((2, rank, rank), f32),
             V((n_dp, BLOCK, depth), bf16),
-            V((n_dp, BLOCK, depth), bf16),
-            V((share, depth), f32),
-            V((n_dp, share, depth), f32),
+            V((n_dp // 2, BLOCK, depth), bf16),
+            V((n_dp // 2, BLOCK, depth), bf16),
+            V((n_dp // 2, BLOCK, depth), bf16),
+            V((share, depth), bf16),
+            V((n_dp, share, depth), bf16),
             dma((chunks, 2)),
+            dma((CUTS,)), dma((CUTS,)),
             dma((n_dp,)), dma((n_dp,)),
             dma((messages,)), dma((messages,)),
-            dma((n_dp,)), dma((n_dp,)),
+            dma((CUTS * n_dp // 2,)), dma((CUTS * n_dp // 2,)),
             dma((n_dp,)), dma((n_dp,)),
         ],
         compiler_params=pltpu.CompilerParams(
             collective_id=0, has_side_effects=True, vmem_limit_bytes=64_000_000
         ),
         name="dora_pair",
-    )(padded, frozen_weight, adapter_down, adapter_up, magnitude, hidden_gradient, gather_map, scatter_map)
-    return hidden, tgrad, agrad.reshape(2, rank, depth), ugrad, mgrad
+    )(tokens, frozen_weight, adapter_down, adapter_up, magnitude, hidden_gradient, gather_map, scatter_map)
+    return pl.pallas_call(
+        copy_kernel, out_shape=shapes, in_specs=[vmem] * 5, out_specs=(vmem,) * 5, name="hand_over"
+    )(*outs)
 
 
 def per_device(n_dp, n_mp, *arrays):
@@ -464,9 +519,11 @@
     rank, width = adapter_up.shape[1:]
     fits = (
         n_mp == 2
-        and depth % TILE == 0
+        and n_dp % 2 == 0
+        and depth % (CUTS * TILE) == 0
         and width % (CHUNKS * TILE) == 0
         and (2 * rank) % n_dp == 0
+        and rank % (2 * rank // n_dp) == 0
         and t + 2 * rank // n_dp <= BLOCK
         and hidden_gradient.shape[0] % 16 == 0
         and 2 * frozen_weight.size <= 24 * 2**20
@@ -477,6 +534,7 @@
 
 
 CHUNKS = 3
+CUTS = 3
 
 
 def solution(mesh):

time: 137 us -> 102 us (0.74)
  Pallas kernels: 124 us -> 101 us
  local copies, waits for them, and re-layouts: 9.81 us -> 0 us
  other arithmetic: 1.53 us -> 0 us
    pallas_call x1 -> x2, Pallas kernels: 124 us -> 101 us  [the longest x1 99 us: fused_on_device(): pl.pallas_call(functools.partial(fused_kernel, n_dp, chunks), out_shape=s...]
    unnamed x4 -> x0, local copies, waits for them, and re-layouts: 6.4 us -> none
    reshape x1 -> x0, local copies, waits for them, and re-layouts: 1.88 us -> none  [fused_on_device(): return (hidden, tgrad, agrad.reshape(2, rank, depth), ugrad, mgrad)]
    pad x1 -> x0, local copies, waits for them, and re-layouts: 1.53 us -> none  [fused_on_device(): padded = jnp.pad(tokens, ((0, BLOCK - t), (0, 0)))]
    convert_element_type x2 -> x0, other arithmetic: 1.42 us -> none  [the longest x1 0.73 us: fused_on_device(): gather_map = (places[:, None] == slots[None, :]).astype(bf16)]
where the time goes in v2:
time: 102 us
  Pallas kernels  101 us (99%)
    pallas_call x1, Pallas kernels, fused_on_device(): pl.pallas_call(functools.partial(fused_kernel, n_dp, chunks), out_shape=s...  99 us
    pallas_call x1, Pallas kernels, fused_on_device(): pl.pallas_call(copy_kernel, out_shape=shapes, in_specs=[vmem] * 5, out_sp...  2.29 us

profile of v2, /device:TPU:0, one launch (start us, length us, event | category | flops | bytes accessed | tf_op | source)
XLA Modules:
  0.0 101.9 jit_solution(6961194473143517408)
XLA Ops:
  0.6 99.0 %dora_pair.1 = (bf16[96,2304]{1,0:T(8,128)(2,1)}, f32[12,2304]{1,0:T(8,128)}, f32[2,16,2304]{2,1,0:T(8,128)}, f32[2,16,2304]{2,1,0:T(8,128)}, f32[2,2304]{1,0:T(2,128)}) custom-call(bf16[12,2304]{1,0:T(8,128)(2,1)} %tok.1, bf16[2,2304,2304]{2,1,0:T(8,128)(2,1)} %w.1, bf16[2,16,2304]{2,1,0:T(8,128)(2,1)} %ad.1, bf16[2,16,2304]{2,1,0:T(8,128)(2,1)} %up.1, ...), custom_call_target="tpu_custom_call" | custom-call | tf_op jit(solution)/shard_map/dora_pair/pallas_call | solution.py:464
  99.6 2.3 %hand_over.1 = (bf16[96,2304]{1,0:T(8,128)(2,1)}, f32[12,2304]{1,0:T(8,128)}, f32[2,16,2304]{2,1,0:T(8,128)}, f32[2,16,2304]{2,1,0:T(8,128)}, f32[2,2304]{1,0:T(2,128)}) custom-call(bf16[96,2304]{1,0:T(8,128)(2,1)} %get-tuple-element.10.refs_0_, f32[12,2304]{1,0:T(8,128)} %get-tuple-element.11.refs_1_, f32[2,16,2304]{2,1,0:T(8,128)} %get-tuple-element.12.refs_2_, ...), custom_call_target="tpu_custom_call" | custom-call | tf_op jit(solution)/shard_map/hand_over/pallas_call | solution.py:511
